TPU v7x, 32 devices: a whole 2x2x4 slice. The times are simulated.
32 devices in a mesh: section: 2 (over x), shard: 4 (over z), replica: 4 (over y, core).
Axes of the slice: x: 2, y: 2, z: 4, core: 2. Of those that a mesh axis runs over, the one named last changes fastest.
Arguments:
- tokens: bfloat16 [3072, 2048], P(('shard', 'replica')), may hold values from -6 to 6
- targets: bfloat16 [3072, 2048], P(('shard', 'replica')), may hold values from -6 to 6
- deal: int32 [16, 192], P(('shard', 'replica')), may hold values from 0 to 191, each once within a row
- lengths: int32 [32, 2], P(('shard', 'replica')), may hold values from 24 to 48, as said below
- attn_gain: bfloat16 [2, 2048], P('section'), may hold values from 0.5 to 1.5
- w_query: bfloat16 [2, 2048, 2048], P('section', None, 'shard'), may hold values from -0.125 to 0.125
- w_key: bfloat16 [2, 2048, 512], P('section', None, 'shard'), may hold values from -0.125 to 0.125
- w_value: bfloat16 [2, 2048, 512], P('section', None, 'shard'), may hold values from -0.125 to 0.125
- w_out: bfloat16 [2, 2048, 2048], P('section', None, 'shard'), may hold values from -0.5 to 0.5
- ffn_gain: bfloat16 [2, 2048], P('section'), may hold values from 0.5 to 1.5
- w_gate: bfloat16 [2, 2048, 8192], P('section', None, 'shard'), may hold values from -0.125 to 0.125
- w_up: bfloat16 [2, 2048, 8192], P('section', None, 'shard'), may hold values from -0.125 to 0.125
- w_down: bfloat16 [2, 8192, 2048], P('section', 'shard'), may hold values from -0.09375 to 0.09375
Outputs:
- loss: float32 [], replicated
- outputs: bfloat16 [2, 3072, 2048], P('section', ('shard', 'replica'))
- input_grad: bfloat16 [2, 3072, 2048], P('section', ('shard', 'replica'))
- attn_gain_grad: float32 [2, 2048], P('section', ('shard', 'replica'))
- w_query_grad: float32 [2, 2048, 2048], P('section', 'replica', 'shard')
- w_key_grad: float32 [2, 2048, 512], P('section', 'replica', 'shard')
- w_value_grad: float32 [2, 2048, 512], P('section', 'replica', 'shard')
- w_out_grad: float32 [2, 2048, 2048], P('section', 'replica', 'shard')
- ffn_gain_grad: float32 [2, 2048], P('section', ('shard', 'replica'))
- w_gate_grad: float32 [2, 2048, 8192], P('section', 'replica', 'shard')
- w_up_grad: float32 [2, 2048, 8192], P('section', 'replica', 'shard')
- w_down_grad: float32 [2, 8192, 2048], P('section', 'shard', 'replica')
Inputs may be any that keep to these rules, and one draw needn't show every extreme that they name: Each row of deal is a permutation of 0 to 191. Row b * 2 + m holds the lengths of the sequences packed, in order from row 0, into micro-batch m of token block b; the rest of the slot is padding.
All inputs are finite; a program needn't handle non-finite values.
Results may differ from a plain program's by a relative error of at most 0.028.
Values may be sent and summed in bfloat16 or wider, within the bound.
A program may use at most 256 MiB of HBM per device.

v0:
```python
import jax
import jax.numpy as jnp
from jax import lax
from jax.sharding import PartitionSpec as P

H = 32
KV = 8
HD = 64


EPS = 1e-05
NEG = -1e30
ROPE_BASE = 500000.0


def from_behind(block, axis, distance):
    devices = range(lax.axis_size(axis))
    route = [(i - distance, i) for i in devices if i - distance in devices]
    return lax.ppermute(block, axis, route)


def layout(seq_lengths, row_count):
    row_index = jnp.arange(row_count, dtype=jnp.int32)
    ends = jnp.cumsum(seq_lengths)
    segment = jnp.sum((row_index[:, None] >= ends[None, :]).astype(jnp.int32), axis=1)
    begins = jnp.concatenate([jnp.zeros((1,), jnp.int32), ends])
    pick = (segment[:, None] == jnp.arange(begins.shape[0], dtype=jnp.int32)[None, :]).astype(
        jnp.int32
    )
    position = row_index - jnp.sum(pick * begins[None, :], axis=1)
    return (segment, position)


def rope_tables(position, width):
    half = width // 2
    freq = ROPE_BASE ** (-2.0 * jnp.arange(half, dtype=jnp.float32) / width)
    angle = position.astype(jnp.float32)[..., None] * freq
    return (jnp.cos(angle), jnp.sin(angle))


def rotate(vector, cosine, sine):
    half = vector.shape[-1] // 2
    first_half, second_half = (vector[..., :half], vector[..., half:])
    return jnp.concatenate(
        [first_half * cosine - second_half * sine, second_half * cosine + first_half * sine],
        axis=-1,
    )


def rotate_back(grad, cosine, sine):
    half = grad.shape[-1] // 2
    first_half, second_half = (grad[..., :half], grad[..., half:])
    return jnp.concatenate(
        [first_half * cosine + second_half * sine, second_half * cosine - first_half * sine],
        axis=-1,
    )


def across(left, right):
    return lax.dot_general(
        left, right, (((1,), (1,)), ((), ())), preferred_element_type=jnp.float32
    )


def down_rows(left, right):
    return lax.dot_general(
        left, right, (((0,), (0,)), ((), ())), preferred_element_type=jnp.float32
    )


def attend_mask(seq_lengths, row_count):
    segment, position = layout(seq_lengths, row_count)
    row_index = jnp.arange(row_count, dtype=jnp.int32)
    allowed = (segment[:, None] == segment[None, :]) & (row_index[:, None] >= row_index[None, :])
    cosine, sine = rope_tables(position, HD)
    return (allowed, cosine[:, None, :], sine[:, None, :])


def owned(grad, split_more):
    portion = lax.psum_scatter(
        grad.astype(jnp.bfloat16), "replica", scatter_dimension=0, tiled=True
    ).astype(jnp.float32)
    if split_more:
        portion = lax.psum_scatter(
            portion.astype(jnp.bfloat16), "shard", scatter_dimension=1, tiled=True
        ).astype(jnp.float32)
    return portion


def per_device(
    tokens,
    targets,
    deal,
    lengths,
    attn_gain,
    w_query,
    w_key,
    w_value,
    w_out,
    ffn_gain,
    w_gate,
    w_up,
    w_down,
):
    f32 = jnp.float32
    bf16 = jnp.bfloat16
    section_id = lax.axis_index("section")
    later = section_id == 1
    micro_count = lengths.shape[0]
    row_count = tokens.shape[0] // micro_count
    model_width = tokens.shape[1]
    group_size = H // KV
    score_scale = HD ** (-0.5)
    arrival = deal[0]
    slot_inputs = tokens[arrival].reshape(micro_count, row_count, model_width)
    teacher = targets[arrival].astype(f32)
    gain_attn = attn_gain[0].astype(f32)
    gain_ffn = ffn_gain[0].astype(f32)
    w_q, w_k, w_v, w_o = (
        lax.all_gather(w_query[0], "shard", axis=1, tiled=True),
        lax.all_gather(w_key[0], "shard", axis=1, tiled=True),
        lax.all_gather(w_value[0], "shard", axis=1, tiled=True),
        lax.all_gather(w_out[0], "shard", axis=1, tiled=True),
    )
    w_g, w_u, w_d = (w_gate[0], w_up[0], w_down[0])
    received = jnp.zeros((row_count, model_width), bf16)
    outputs_seen = []
    kept_seen = []
    for moment in range(micro_count + 1):
        own_batch = jnp.clip(moment - section_id, 0, micro_count - 1)
        fresh = lax.dynamic_index_in_dim(slot_inputs, own_batch, 0, keepdims=False)
        seq_lengths = lax.dynamic_index_in_dim(lengths, own_batch, 0, keepdims=False)
        rows_in = jnp.where(later, received, fresh).astype(f32)
        forward_allowed, forward_cosine, forward_sine = attend_mask(seq_lengths, row_count)
        forward_inverse_one = lax.rsqrt(jnp.mean(rows_in * rows_in, axis=1, keepdims=True) + EPS)
        forward_normed_one = (rows_in * forward_inverse_one * gain_attn).astype(bf16)
        query = jnp.dot(forward_normed_one, w_q, preferred_element_type=f32).reshape(
            row_count, H, HD
        )
        keys = jnp.dot(forward_normed_one, w_k, preferred_element_type=f32).reshape(
            row_count, KV, HD
        )
        forward_values = (
            jnp.dot(forward_normed_one, w_v, preferred_element_type=f32)
            .astype(bf16)
            .reshape(row_count, KV, HD)
        )
        forward_q_rot = (
            rotate(query, forward_cosine, forward_sine)
            .astype(bf16)
            .reshape(row_count, KV, group_size, HD)
        )
        forward_k_rot = rotate(keys, forward_cosine, forward_sine).astype(bf16)
        forward_scores = (
            jnp.einsum("rkgd,skd->kgrs", forward_q_rot, forward_k_rot, preferred_element_type=f32)
            * score_scale
        )
        forward_scores = jnp.where(forward_allowed, forward_scores, NEG)
        highest = jnp.max(forward_scores, axis=-1, keepdims=True)
        raised = jnp.exp(forward_scores - highest)
        totals = jnp.sum(raised, axis=-1, keepdims=True)
        forward_probs = (raised / totals).astype(bf16)
        forward_log_total = highest + jnp.log(totals)
        forward_mixed = jnp.einsum(
            "kgrs,skd->rkgd", forward_probs, forward_values, preferred_element_type=f32
        )
        forward_mixed = forward_mixed.reshape(row_count, H * HD).astype(bf16)
        forward_hidden = rows_in + jnp.dot(forward_mixed, w_o, preferred_element_type=f32)
        forward_inverse_two = lax.rsqrt(
            jnp.mean(forward_hidden * forward_hidden, axis=1, keepdims=True) + EPS
        )
        forward_normed_two = (forward_hidden * forward_inverse_two * gain_ffn).astype(bf16)
        ffn_spread = lax.all_gather(forward_normed_two, "shard", axis=0, tiled=True)
        ffn_gate_pre = jnp.dot(ffn_spread, w_g, preferred_element_type=f32)
        ffn_up_pre = jnp.dot(ffn_spread, w_u, preferred_element_type=f32)
        ffn_active = (jax.nn.silu(ffn_gate_pre) * ffn_up_pre).astype(bf16)
        branch = lax.psum_scatter(
            jnp.dot(ffn_active, w_d, preferred_element_type=f32).astype(jnp.bfloat16),
            "shard",
            scatter_dimension=0,
            tiled=True,
        ).astype(jnp.float32)
        forward_kept = (
            rows_in.astype(bf16),
            forward_inverse_one,
            forward_normed_one,
            forward_q_rot,
            forward_k_rot,
            forward_values,
            forward_log_total,
            forward_mixed,
            forward_hidden,
            forward_inverse_two,
            ffn_spread,
            ffn_gate_pre,
            ffn_up_pre,
            ffn_active,
        )
        result = forward_hidden + branch
        kept = forward_kept
        if moment < micro_count:
            received = from_behind(result.astype(bf16), "section", 1)
        outputs_seen.append(result)
        kept_seen.append(kept)
    mine = lax.dynamic_slice_in_dim(jnp.stack(outputs_seen), section_id, micro_count, 0).reshape(
        -1, model_width
    )
    segments_all = jax.vmap(lambda seq_lengths: layout(seq_lengths, row_count)[0])(lengths)
    valid_rows = (segments_all < lengths.shape[1]).reshape(-1).astype(f32)[:, None]
    errors = mine - teacher
    switch = later.astype(f32)
    local_square = jnp.sum(valid_rows * errors * errors) * switch
    local_count = jnp.sum(lengths).astype(f32) * switch
    total_square, total_count = lax.psum(
        (local_square, local_count), ("section", "shard", "replica")
    )
    loss_value = total_square / (total_count * model_width)
    all_tokens = tokens.shape[0] * lax.axis_size("shard") * lax.axis_size("replica")
    grad_final = (all_tokens / total_count * errors * valid_rows).reshape(
        micro_count, row_count, model_width
    )
    stacked_kept = jax.tree.map(lambda *pieces: jnp.stack(pieces), *kept_seen)
    coming = jnp.zeros((row_count, model_width), bf16)
    sent_seen = []
    stored_seen = []
    gain_attn_total = jnp.zeros((model_width,), f32)
    gain_ffn_total = jnp.zeros((model_width,), f32)
    for moment in range(micro_count + 1):
        raw_batch = moment - 1 + section_id
        own_batch = jnp.clip(raw_batch, 0, micro_count - 1)
        kept = jax.tree.map(
            lambda arrays: lax.dynamic_index_in_dim(
                arrays, own_batch + section_id, 0, keepdims=False
            ),
            stacked_kept,
        )
        seq_lengths = lax.dynamic_index_in_dim(lengths, own_batch, 0, keepdims=False)
        final_rows = lax.dynamic_index_in_dim(grad_final, own_batch, 0, keepdims=False)
        incoming = jnp.where(later, final_rows, coming.astype(f32))
        (
            input_rows,
            inverse_one,
            normed_one,
            q_rot,
            k_rot,
            values,
            log_total,
            mixed,
            hidden,
            inverse_two,
            spread,
            gate_pre,
            up_pre,
            active,
        ) = kept
        allowed, cosine, sine = attend_mask(seq_lengths, row_count)
        grad_branch = incoming.astype(bf16)
        backward_grad_rows = lax.all_gather(grad_branch, "shard", axis=0, tiled=True)
        grad_active = across(backward_grad_rows, w_d)
        sigma = jax.nn.sigmoid(gate_pre)
        backward_grad_gate = (
            grad_active * up_pre * sigma * (1.0 + gate_pre * (1.0 - sigma))
        ).astype(bf16)
        backward_grad_up = (grad_active * gate_pre * sigma).astype(bf16)
        grad_normed = lax.psum_scatter(
            (across(backward_grad_gate, w_g) + across(backward_grad_up, w_u)).astype(jnp.bfloat16),
            "shard",
            scatter_dimension=0,
            tiled=True,
        ).astype(jnp.float32)
        scaled_two = hidden * inverse_two
        gain_ffn_part = jnp.sum(grad_normed * scaled_two, axis=0)
        pushed_two = grad_normed * gain_ffn
        grad_hidden = incoming + inverse_two * (
            pushed_two - scaled_two * jnp.mean(pushed_two * scaled_two, axis=1, keepdims=True)
        )
        backward_grad_attn = grad_hidden.astype(bf16)
        grad_mixed = (
            across(backward_grad_attn, w_o).astype(bf16).reshape(row_count, KV, group_size, HD)
        )
        scores = (
            jnp.einsum("rkgd,skd->kgrs", q_rot, k_rot, preferred_element_type=f32) * score_scale
        )
        probs = jnp.where(allowed, jnp.exp(scores - log_total), 0.0)
        grad_probs = jnp.einsum("rkgd,skd->kgrs", grad_mixed, values, preferred_element_type=f32)
        grad_scores = (
            probs * (grad_probs - jnp.sum(grad_probs * probs, axis=-1, keepdims=True))
        ).astype(bf16)
        grad_qrot = (
            jnp.einsum("kgrs,skd->rkgd", grad_scores, k_rot, preferred_element_type=f32)
            * score_scale
        )
        grad_krot = (
            jnp.einsum("kgrs,rkgd->skd", grad_scores, q_rot, preferred_element_type=f32)
            * score_scale
        )
        backward_grad_values = jnp.einsum(
            "kgrs,rkgd->skd", probs.astype(bf16), grad_mixed, preferred_element_type=f32
        )
        backward_grad_values = backward_grad_values.astype(bf16).reshape(row_count, KV * HD)
        backward_grad_query = (
            rotate_back(grad_qrot.reshape(row_count, H, HD), cosine, sine)
            .astype(bf16)
            .reshape(row_count, H * HD)
        )
        backward_grad_keys = (
            rotate_back(grad_krot, cosine, sine).astype(bf16).reshape(row_count, KV * HD)
        )
        grad_normed_one = (
            across(backward_grad_query, w_q)
            + across(backward_grad_keys, w_k)
            + across(backward_grad_values, w_v)
        )
        scaled_one = input_rows.astype(f32) * inverse_one
        gain_attn_part = jnp.sum(grad_normed_one * scaled_one, axis=0)
        pushed_one = grad_normed_one * gain_attn
        grad_input = grad_hidden + inverse_one * (
            pushed_one - scaled_one * jnp.mean(pushed_one * scaled_one, axis=1, keepdims=True)
        )
        stored = (
            normed_one,
            backward_grad_query,
            backward_grad_keys,
            backward_grad_values,
            mixed,
            backward_grad_attn,
            spread,
            backward_grad_gate,
            backward_grad_up,
            backward_grad_rows,
            active,
        )
        grad_input, stored, gain_attn_part, gain_ffn_part = (
            grad_input,
            stored,
            gain_attn_part,
            gain_ffn_part,
        )
        active_moment = ((raw_batch >= 0) & (raw_batch < micro_count)).astype(f32)
        gain_attn_total = gain_attn_total + active_moment * gain_attn_part
        gain_ffn_total = gain_ffn_total + active_moment * gain_ffn_part
        sent = grad_input.astype(bf16)
        if moment < micro_count:
            coming = from_behind(sent, "section", -1)
        sent_seen.append(sent)
        stored_seen.append(stored)
    first_moment = 1 - section_id
    grads_in = lax.dynamic_slice_in_dim(jnp.stack(sent_seen), first_moment, micro_count, 0).reshape(
        -1, model_width
    )
    stacked_stored = jax.tree.map(lambda *pieces: jnp.stack(pieces), *stored_seen)
    stored_valid = jax.tree.map(
        lambda arrays: lax.dynamic_slice_in_dim(arrays, first_moment, micro_count, 0).reshape(
            (-1,) + arrays.shape[2:]
        ),
        stacked_stored,
    )
    (
        normed_rows,
        grad_query,
        grad_keys,
        grad_values,
        mixed_rows,
        grad_attn,
        spread_rows,
        grad_gate,
        grad_up,
        grad_rows,
        active_rows,
    ) = stored_valid
    query_grad = owned(down_rows(normed_rows, grad_query), True)
    key_grad = owned(down_rows(normed_rows, grad_keys), True)
    value_grad = owned(down_rows(normed_rows, grad_values), True)
    out_grad = owned(down_rows(mixed_rows, grad_attn), True)
    gate_grad = owned(down_rows(spread_rows, grad_gate), False)
    up_grad = owned(down_rows(spread_rows, grad_up), False)
    down_grad = owned(down_rows(grad_rows, active_rows), False).T
    attn_gain_part, ffn_gain_part = (
        lax.psum_scatter(gain_attn_total, ("shard", "replica"), scatter_dimension=0, tiled=True),
        lax.psum_scatter(gain_ffn_total, ("shard", "replica"), scatter_dimension=0, tiled=True),
    )
    outputs_local = (
        jnp.zeros((tokens.shape[0], model_width), bf16).at[arrival].set(mine.astype(bf16))[None]
    )
    input_local = jnp.zeros((tokens.shape[0], model_width), bf16).at[arrival].set(grads_in)[None]
    return (
        loss_value,
        outputs_local,
        input_local,
        attn_gain_part[None],
        query_grad[None],
        key_grad[None],
        value_grad[None],
        out_grad[None],
        ffn_gain_part[None],
        gate_grad[None],
        up_grad[None],
        down_grad[None],
    )


def solution(mesh):
    in_specs = (
        P(("shard", "replica"), None),
        P(("shard", "replica"), None),
        P(("shard", "replica"), None),
        P(("shard", "replica"), None),
        P("section", None),
        P("section", None, "shard"),
        P("section", None, "shard"),
        P("section", None, "shard"),
        P("section", None, "shard"),
        P("section", None),
        P("section", None, "shard"),
        P("section", None, "shard"),
        P("section", "shard", None),
    )
    out_specs = (
        P(),
        P("section", ("shard", "replica"), None),
        P("section", ("shard", "replica"), None),
        P("section", ("shard", "replica")),
        P("section", "replica", "shard"),
        P("section", "replica", "shard"),
        P("section", "replica", "shard"),
        P("section", "replica", "shard"),
        P("section", ("shard", "replica")),
        P("section", "replica", "shard"),
        P("section", "replica", "shard"),
        P("section", "shard", "replica"),
    )
    return jax.shard_map(
        per_device, mesh=mesh, in_specs=in_specs, out_specs=out_specs, check_vma=False
    )
```

profile of v0, /device:TPU:0, one launch (start us, length us, event | category | flops | bytes accessed | tf_op | source)
XLA Modules:
  0.0 1781.9 jit_solution(15175932796307633958)
XLA Ops:
  16.5 42.1 %all-gather.27.cloned.1.call-done = bf16[1,2048,512]{2,1,0:T(8,128)(2,1)} async-done(((bf16[1,2048,128]{2,1,0:T(8,128)(2,1)}), bf16[1,2048,512]{2,1,0:T(8,128)(2,1)}) %all-gather.27.cloned.1.call-update) | async-done | bytes 2097168 | tf_op jit(solution)/shard_map/all_gather | solution.py:122
  60.8 43.8 %all-gather.29.cloned.1.call-done = bf16[1,2048,512]{2,1,0:T(8,128)(2,1)} async-done(((bf16[1,2048,128]{2,1,0:T(8,128)(2,1)}), bf16[1,2048,512]{2,1,0:T(8,128)(2,1)}) %all-gather.29.cloned.1.call-update) | async-done | bytes 2097168 | tf_op jit(solution)/shard_map/all_gather | solution.py:121
  108.4 145.7 %all-gather.31.cloned.1.call-done = bf16[1,2048,2048]{2,1,0:T(8,128)(2,1)} async-done(((bf16[1,2048,512]{2,1,0:T(8,128)(2,1)}), bf16[1,2048,2048]{2,1,0:T(8,128)(2,1)}) %all-gather.31.cloned.1.call-update) | async-done | bytes 8388624 | tf_op jit(solution)/shard_map/all_gather | solution.py:120
  254.0 12.5 copy.169
  274.1 129.2 %all-gather.33.cloned.1.call-done = bf16[1,2048,2048]{2,1,0:T(8,128)(2,1)} async-done(((bf16[1,2048,512]{2,1,0:T(8,128)(2,1)}), bf16[1,2048,2048]{2,1,0:T(8,128)(2,1)}) %all-gather.33.cloned.1.call-update) | async-done | bytes 8388624 | tf_op jit(solution)/shard_map/all_gather | solution.py:123
  410.0 35.1 %all-gather.15.cloned.1.call-done = bf16[384,2048]{1,0:T(8,128)(2,1)} async-done(((bf16[96,2048]{1,0:T(8,128)(2,1)}), bf16[384,2048]{1,0:T(8,128)(2,1)}) %all-gather.15.cloned.1.call-update) | async-done | bytes 1572880 | tf_op jit(solution)/shard_map/all_gather | solution.py:173
  468.1 34.4 %reduce-scatter.22.cloned.1.call-done = bf16[96,2048]{1,0:T(8,128)(2,1)} async-done(((bf16[384,2048]{1,0:T(8,128)(2,1)}), bf16[96,2048]{1,0:T(8,128)(2,1)}) %reduce-scatter.22.cloned.1.call-update) | async-done | bytes 393232 | tf_op jit(solution)/shard_map/reduce_scatter | solution.py:177
  534.1 36.9 %all-gather.17.cloned.1.call-done = bf16[384,2048]{1,0:T(8,128)(2,1)} async-done(((bf16[96,2048]{1,0:T(8,128)(2,1)}), bf16[384,2048]{1,0:T(8,128)(2,1)}) %all-gather.17.cloned.1.call-update) | async-done | bytes 1572880 | tf_op jit(solution)/shard_map/all_gather | solution.py:173
  593.9 34.4 %reduce-scatter.24.cloned.1.call-done = bf16[96,2048]{1,0:T(8,128)(2,1)} async-done(((bf16[384,2048]{1,0:T(8,128)(2,1)}), bf16[96,2048]{1,0:T(8,128)(2,1)}) %reduce-scatter.24.cloned.1.call-update) | async-done | bytes 393232 | tf_op jit(solution)/shard_map/reduce_scatter | solution.py:177
  659.7 37.1 %all-gather.19.cloned.1.call-done = bf16[384,2048]{1,0:T(8,128)(2,1)} async-done(((bf16[96,2048]{1,0:T(8,128)(2,1)}), bf16[384,2048]{1,0:T(8,128)(2,1)}) %all-gather.19.cloned.1.call-update) | async-done | bytes 1572880 | tf_op jit(solution)/shard_map/all_gather | solution.py:173
  723.6 30.7 %reduce-scatter.26.cloned.1.call-done = bf16[96,2048]{1,0:T(8,128)(2,1)} async-done(((bf16[384,2048]{1,0:T(8,128)(2,1)}), bf16[96,2048]{1,0:T(8,128)(2,1)}) %reduce-scatter.26.cloned.1.call-update) | async-done | bytes 393232 | tf_op jit(solution)/shard_map/reduce_scatter | solution.py:177
  760.4 39.0 %all-reduce.2 = (f32[]{:T(128)}, f32[]{:T(128)}) all-reduce(f32[]{:T(128)S(6)} %mul.1184, f32[]{:T(128)S(6)} %mul.1185), channel_id=1, replica_groups=mesh['section'=2,'shard'=4,'replica'=4] {'section','shard','replica'}, use_global_device_ids=true, to_apply=%region_27.28 | all-reduce | flops 2 | bytes 16 | tf_op jit(solution)/shard_map/psum | solution.py:214
  817.3 23.7 %all-gather.21.cloned.1.call-done = bf16[384,2048]{1,0:T(8,128)(2,1)} async-done(((bf16[96,2048]{1,0:T(8,128)(2,1)}), bf16[384,2048]{1,0:T(8,128)(2,1)}) %all-gather.21.cloned.1.call-update) | async-done | bytes 1572880 | tf_op jit(solution)/shard_map/all_gather | solution.py:258
  880.4 22.6 %reduce-scatter.28.cloned.1.call-done = bf16[96,2048]{1,0:T(8,128)(2,1)} async-done(((bf16[384,2048]{1,0:T(8,128)(2,1)}), bf16[96,2048]{1,0:T(8,128)(2,1)}) %reduce-scatter.28.cloned.1.call-update) | async-done | bytes 393232 | tf_op jit(solution)/shard_map/reduce_scatter | solution.py:265
  931.4 11.0 collective-permute-done.2
  944.8 35.2 %all-gather.23.cloned.1.call-done = bf16[384,2048]{1,0:T(8,128)(2,1)} async-done(((bf16[96,2048]{1,0:T(8,128)(2,1)}), bf16[384,2048]{1,0:T(8,128)(2,1)}) %all-gather.23.cloned.1.call-update) | async-done | bytes 1572880 | tf_op jit(solution)/shard_map/all_gather | solution.py:258
  1007.7 34.1 %reduce-scatter.30.cloned.1.call-done = bf16[96,2048]{1,0:T(8,128)(2,1)} async-done(((bf16[384,2048]{1,0:T(8,128)(2,1)}), bf16[96,2048]{1,0:T(8,128)(2,1)}) %reduce-scatter.30.cloned.1.call-update) | async-done | bytes 393232 | tf_op jit(solution)/shard_map/reduce_scatter | solution.py:265
  1066.8 11.0 collective-permute-done.3
  1080.3 35.2 %all-gather.25.cloned.1.call-done = bf16[384,2048]{1,0:T(8,128)(2,1)} async-done(((bf16[96,2048]{1,0:T(8,128)(2,1)}), bf16[384,2048]{1,0:T(8,128)(2,1)}) %all-gather.25.cloned.1.call-update) | async-done | bytes 1572880 | tf_op jit(solution)/shard_map/all_gather | solution.py:258
  1147.3 30.0 %reduce-scatter.32.cloned.1.call-done = bf16[96,2048]{1,0:T(8,128)(2,1)} async-done(((bf16[384,2048]{1,0:T(8,128)(2,1)}), bf16[96,2048]{1,0:T(8,128)(2,1)}) %reduce-scatter.32.cloned.1.call-update) | async-done | bytes 393232 | tf_op jit(solution)/shard_map/reduce_scatter | solution.py:265
  1243.0 22.3 %reduce-scatter.40.cloned.1.call-done = bf16[512,512]{1,0:T(8,128)(2,1)} async-done(((bf16[2048,512]{1,0:T(8,128)(2,1)}), bf16[512,512]{1,0:T(8,128)(2,1)}) %reduce-scatter.40.cloned.1.call-update) | async-done | bytes 524304 | tf_op jit(solution)/shard_map/reduce_scatter | solution.py:80
  1271.2 11.5 bitcast_convert_fusion
  1289.6 11.5 bitcast_convert_fusion.2
  1301.2 13.3 bitcast_convert_fusion.1
  1314.6 24.6 %reduce-scatter.42.cloned.1.call-done = bf16[512,2048]{1,0:T(8,128)(2,1)} async-done(((bf16[2048,2048]{1,0:T(8,128)(2,1)}), bf16[512,2048]{1,0:T(8,128)(2,1)}) %reduce-scatter.42.cloned.1.call-update) | async-done | bytes 2097168 | tf_op jit(solution)/shard_map/reduce_scatter | solution.py:80
  1356.1 57.0 %reduce-scatter.34.cloned.1.call-done = bf16[512,2048]{1,0:T(8,128)(2,1)} async-done(((bf16[2048,2048]{1,0:T(8,128)(2,1)}), bf16[512,2048]{1,0:T(8,128)(2,1)}) %reduce-scatter.34.cloned.1.call-update) | async-done | bytes 2097168 | tf_op jit(solution)/shard_map/reduce_scatter | solution.py:80
  1417.8 60.3 %all-reduce.3 = (f32[2048]{0:T(1024)S(1)}, f32[2048]{0:T(1024)S(1)}) all-reduce(f32[2048]{0:T(1024)S(1)} %multiply_add_fusion.7, f32[2048]{0:T(1024)S(1)} %multiply_add_fusion.6), channel_id=12, replica_groups=mesh['section'=2,'shard'=4,'replica'=4] {'shard','replica'}, use_global_device_ids=true, to_apply=%region_56.57.clone | all-reduce | flops 4096 | bytes 32768
  1482.9 49.8 %reduce-scatter.50.cloned.1.call-done = bf16[512,2048]{1,0:T(8,128)(2,1)} async-done(((bf16[2048,2048]{1,0:T(8,128)(2,1)}), bf16[512,2048]{1,0:T(8,128)(2,1)}) %reduce-scatter.50.cloned.1.call-update) | async-done | bytes 2097168 | tf_op jit(solution)/shard_map/reduce_scatter | solution.py:80
  1542.1 64.4 %reduce-scatter.46.cloned.1.call-done = bf16[512,2048]{1,0:T(8,128)(2,1)} async-done(((bf16[2048,2048]{1,0:T(8,128)(2,1)}), bf16[512,2048]{1,0:T(8,128)(2,1)}) %reduce-scatter.46.cloned.1.call-update) | async-done | bytes 2097168 | tf_op jit(solution)/shard_map/reduce_scatter | solution.py:80
  1610.6 69.9 %reduce-scatter.48.cloned.1.call-done = bf16[512,2048]{1,0:T(8,128)(2,1)} async-done(((bf16[2048,2048]{1,0:T(8,128)(2,1)}), bf16[512,2048]{1,0:T(8,128)(2,1)}) %reduce-scatter.48.cloned.1.call-update) | async-done | bytes 2097168 | tf_op jit(solution)/shard_map/reduce_scatter | solution.py:80
  1684.7 41.6 %reduce-scatter.44.cloned.1.call-done = bf16[512,512]{1,0:T(8,128)(2,1)} async-done(((bf16[512,2048]{1,0:T(8,128)(2,1)}), bf16[512,512]{1,0:T(8,128)(2,1)}) %reduce-scatter.44.cloned.1.call-update) | async-done | bytes 524304 | tf_op jit(solution)/shard_map/reduce_scatter | solution.py:84
  1728.5 42.9 %reduce-scatter.36.cloned.1.call-done = bf16[512,512]{1,0:T(8,128)(2,1)} async-done(((bf16[512,2048]{1,0:T(8,128)(2,1)}), bf16[512,512]{1,0:T(8,128)(2,1)}) %reduce-scatter.36.cloned.1.call-update) | async-done | bytes 524304 | tf_op jit(solution)/shard_map/reduce_scatter | solution.py:84
  (719 shorter events, 466.1 us)
Async XLA Ops:
  7.2 51.4 %all-gather.27.cloned.1.call-start = ((), (), s32[]{:S(2)}) async-start(), calls=%async_computation.38 | async-start | bytes 2621440 | tf_op jit(solution)/shard_map/all_gather | solution.py:122
  7.9 96.7 %all-gather.29.cloned.1.call-start = ((), (), s32[]{:S(2)}) async-start(), calls=%async_computation.39 | async-start | bytes 2621440 | tf_op jit(solution)/shard_map/all_gather | solution.py:121
  8.7 245.3 %all-gather.31.cloned.1.call-start = ((), (), s32[]{:S(2)}) async-start(), calls=%async_computation.40 | async-start | bytes 10485760 | tf_op jit(solution)/shard_map/all_gather | solution.py:120
  9.5 393.8 %all-gather.33.cloned.1.call-start = ((), (), s32[]{:S(2)}) async-start(), calls=%async_computation.41 | async-start | bytes 10485760 | tf_op jit(solution)/shard_map/all_gather | solution.py:123
  10.0 435.1 %all-gather.15.cloned.1.call-start = ((), (), s32[]{:S(2)}) async-start(), calls=%async_computation.17 | async-start | bytes 1966080 | tf_op jit(solution)/shard_map/all_gather | solution.py:173
  12.7 390.6 %copy-start.23 = (bf16[1,96,2048]{2,1,0:T(8,128)(2,1)}, bf16[1,96,2048]{2,1,0:T(8,128)(2,1)S(1)}, u32[]{:S(2)}) copy-start(bf16[1,96,2048]{2,1,0:T(8,128)(2,1)S(1)} %get-tuple-element.89) | copy-start | bytes 1179652
  409.8 92.7 %reduce-scatter.22.cloned.1.call-start = ((), (), s32[]{:S(2)}) async-start(), calls=%async_computation.18 | async-start | bytes 1966080 | tf_op jit(solution)/shard_map/reduce_scatter | solution.py:177
  468.0 102.9 %all-gather.17.cloned.1.call-start = ((), (), s32[]{:S(2)}) async-start(), calls=%async_computation.19 | async-start | bytes 1966080 | tf_op jit(solution)/shard_map/all_gather | solution.py:173
  504.5 11.3 collective-permute-start
  533.5 94.8 %reduce-scatter.24.cloned.1.call-start = ((), (), s32[]{:S(2)}) async-start(), calls=%async_computation.20 | async-start | bytes 1966080 | tf_op jit(solution)/shard_map/reduce_scatter | solution.py:177
  593.9 102.9 %all-gather.19.cloned.1.call-start = ((), (), s32[]{:S(2)}) async-start(), calls=%async_computation.21 | async-start | bytes 1966080 | tf_op jit(solution)/shard_map/all_gather | solution.py:173
  630.4 11.3 collective-permute-start.1
  659.5 94.9 %reduce-scatter.26.cloned.1.call-start = ((), (), s32[]{:S(2)}) async-start(), calls=%async_computation.22 | async-start | bytes 1966080 | tf_op jit(solution)/shard_map/reduce_scatter | solution.py:177
  719.9 121.1 %all-gather.21.cloned.1.call-start = ((), (), s32[]{:S(2)}) async-start(), calls=%async_computation.23 | async-start | bytes 1966080 | tf_op jit(solution)/shard_map/all_gather | solution.py:258
  803.8 99.3 %reduce-scatter.28.cloned.1.call-start = ((), (), s32[]{:S(2)}) async-start(), calls=%async_computation.24 | async-start | bytes 1966080 | tf_op jit(solution)/shard_map/reduce_scatter | solution.py:265
  868.5 111.4 %all-gather.23.cloned.1.call-start = ((), (), s32[]{:S(2)}) async-start(), calls=%async_computation.25 | async-start | bytes 1966080 | tf_op jit(solution)/shard_map/all_gather | solution.py:258
  930.1 12.3 collective-permute-start.2
  944.5 97.2 %reduce-scatter.30.cloned.1.call-start = ((), (), s32[]{:S(2)}) async-start(), calls=%async_computation.26 | async-start | bytes 1966080 | tf_op jit(solution)/shard_map/reduce_scatter | solution.py:265
  1007.3 108.2 %all-gather.25.cloned.1.call-start = ((), (), s32[]{:S(2)}) async-start(), calls=%async_computation.27 | async-start | bytes 1966080 | tf_op jit(solution)/shard_map/all_gather | solution.py:258
  1065.5 12.3 collective-permute-start.3
  1080.0 97.3 %reduce-scatter.32.cloned.1.call-start = ((), (), s32[]{:S(2)}) async-start(), calls=%async_computation.28 | async-start | bytes 1966080 | tf_op jit(solution)/shard_map/reduce_scatter | solution.py:265
  1142.8 92.7 %reduce-scatter.38.cloned.1.call-start = ((), (), s32[]{:S(2)}) async-start(), calls=%async_computation.31 | async-start | bytes 2621440 | tf_op jit(solution)/shard_map/reduce_scatter | solution.py:80
  1200.8 64.4 %reduce-scatter.40.cloned.1.call-start = ((), (), s32[]{:S(2)}) async-start(), calls=%async_computation.32 | async-start | bytes 2621440 | tf_op jit(solution)/shard_map/reduce_scatter | solution.py:80
  1208.2 131.0 %reduce-scatter.42.cloned.1.call-start = ((), (), s32[]{:S(2)}) async-start(), calls=%async_computation.33 | async-start | bytes 10485760 | tf_op jit(solution)/shard_map/reduce_scatter | solution.py:80
  1221.7 191.4 %reduce-scatter.34.cloned.1.call-start = ((), (), s32[]{:S(2)}) async-start(), calls=%async_computation.29 | async-start | bytes 10485760 | tf_op jit(solution)/shard_map/reduce_scatter | solution.py:80
  1235.4 243.9 %reduce-scatter.52.cloned.1.call-start = ((), (), s32[]{:S(2)}) async-start(), calls=%async_computation.42 | async-start | bytes 655360
  1237.6 242.8 %reduce-scatter.54.cloned.1.call-start = ((), (), s32[]{:S(2)}) async-start(), calls=%async_computation.43 | async-start | bytes 655360
  1267.3 265.3 %reduce-scatter.50.cloned.1.call-start = ((), (), s32[]{:S(2)}) async-start(), calls=%async_computation.37 | async-start | bytes 10485760 | tf_op jit(solution)/shard_map/reduce_scatter | solution.py:80
  1282.7 323.8 %reduce-scatter.46.cloned.1.call-start = ((), (), s32[]{:S(2)}) async-start(), calls=%async_computation.35 | async-start | bytes 10485760 | tf_op jit(solution)/shard_map/reduce_scatter | solution.py:80
  1301.1 379.4 %reduce-scatter.48.cloned.1.call-start = ((), (), s32[]{:S(2)}) async-start(), calls=%async_computation.36 | async-start | bytes 10485760 | tf_op jit(solution)/shard_map/reduce_scatter | solution.py:80
  1314.5 411.8 %reduce-scatter.44.cloned.1.call-start = ((), (), s32[]{:S(2)}) async-start(), calls=%async_computation.34 | async-start | bytes 2621440 | tf_op jit(solution)/shard_map/reduce_scatter | solution.py:84
  1339.3 432.1 %reduce-scatter.36.cloned.1.call-start = ((), (), s32[]{:S(2)}) async-start(), calls=%async_computation.30 | async-start | bytes 2621440 | tf_op jit(solution)/shard_map/reduce_scatter | solution.py:84
  (204 other events, 2931.6 us)
Sparse Core Ops, SparseCore 0:
  9.6 48.9 all-gather.26
  60.1 44.4 all-gather.28
  106.2 147.7 all-gather.30
  255.4 147.7 all-gather.32
  409.9 35.1 all-gather.14
  468.1 34.2 reduce-scatter.21
  533.7 37.2 all-gather.16
  594.0 34.2 reduce-scatter.23
  659.6 37.2 all-gather.18
  720.0 34.3 reduce-scatter.25
  803.9 37.0 all-gather.20
  868.7 34.3 reduce-scatter.27
  944.7 35.2 all-gather.22
  1007.4 34.2 reduce-scatter.29
  1080.1 35.2 all-gather.24
  1142.9 34.2 reduce-scatter.31
  1201.0 30.0 reduce-scatter.37
  1234.0 31.1 reduce-scatter.39
  1267.8 71.3 reduce-scatter.41
  1341.7 71.3 reduce-scatter.33
  1415.9 21.8 reduce-scatter.51
  1440.1 20.2 reduce-scatter.53
  1463.0 69.5 reduce-scatter.49
  1535.1 71.3 reduce-scatter.45
  1609.1 71.3 reduce-scatter.47
  1682.7 43.6 reduce-scatter.43
  1728.5 42.8 reduce-scatter.35
where the time goes:
time: 1790 us; the launch traced here: 1780 us
  waiting for transfers between devices  1160 us (65%)
  matrix products  296 us (17%)
  other arithmetic  103 us (6%)
  blocking collectives  99.3 us (6%)
  local copies, waits for them, and re-layouts  84.8 us (5%)
  between operations  22.8 us (1%)
    reduce_scatter x7, waiting for transfers between devices, owned(): lax.psum_scatter(grad.astype(jnp.bfloat16), 'replica', scatter_dimension=...  288 us
    all_gather x1, waiting for transfers between devices, per_device(): lax.all_gather(w_query[0], 'shard', axis=1, tiled=True)  146 us
    all_gather x1, waiting for transfers between devices, per_device(): lax.all_gather(w_out[0], 'shard', axis=1, tiled=True)  129 us
    dot_general x21, matrix products, across(): lax.dot_general(left, right, (((1,), (1,)), ((), ())), preferred_element_...  122 us
    all_gather x3, waiting for transfers between devices, per_device(): ffn_spread = lax.all_gather(forward_normed_two, 'shard', axis=0, tiled=True)  109 us
    reduce_scatter x3, waiting for transfers between devices, per_device(): lax.psum_scatter(jnp.dot(ffn_active, w_d, preferred_element_type=f32).ast...  99.5 us
    all_gather x3, waiting for transfers between devices, per_device(): lax.all_gather(grad_branch, 'shard', axis=0, tiled=True)  94.1 us
    reduce_scatter x3, waiting for transfers between devices, per_device(): lax.psum_scatter((across(backward_grad_gate, w_g) + across(backward_grad_...  86.7 us
  transfers between devices with their start and end apart: 31, of which 28 were waited for; matrix products, arithmetic and copies ran while one was open for 11% of the time, Pallas kernels for 0%

commit v1 on v0

--- a/solution.py
+++ b/solution.py
@@ -1,6 +1,10 @@
+import functools
+
 import jax
 import jax.numpy as jnp
 from jax import lax
+from jax.experimental import pallas as pl
+from jax.experimental.pallas import tpu as pltpu
 from jax.sharding import PartitionSpec as P
 
 H = 32
@@ -11,6 +15,9 @@
 EPS = 1e-05
 NEG = -1e30
 ROPE_BASE = 500000.0
+MESH = pl.DeviceIdType.MESH
+ANY = pl.BlockSpec(memory_space=pl.ANY)
+VM = pl.BlockSpec(memory_space=pltpu.VMEM)
 
 
 def from_behind(block, axis, distance):
@@ -76,15 +83,320 @@
     return (allowed, cosine[:, None, :], sine[:, None, :])
 
 
-def owned(grad, split_more):
-    portion = lax.psum_scatter(
-        grad.astype(jnp.bfloat16), "replica", scatter_dimension=0, tiled=True
+def place():
+    return (lax.axis_index("section"), lax.axis_index("shard"), lax.axis_index("replica"))
+
+
+def reduce_peers(n_rep):
+    section, shard, replica = place()
+    peers = []
+    bit = 1
+    while bit < n_rep:
+        peers.append((section, shard, replica ^ bit))
+        bit *= 2
+    peers.append((section, shard ^ 1, replica))
+    peers.append((section, 3 - shard, replica))
+    return peers
+
+
+def greet(peers):
+    barrier = pltpu.get_barrier_semaphore()
+    for peer in peers:
+        pl.semaphore_signal(barrier, inc=1, device_id=peer, device_id_type=MESH)
+    pl.semaphore_wait(barrier, len(peers))
+
+
+def butterfly(peers, totals, heard, send_sem, recv_sem):
+    for step, peer in enumerate(peers):
+        copy = pltpu.make_async_remote_copy(
+            src_ref=totals.at[step],
+            dst_ref=heard.at[step],
+            send_sem=send_sem.at[step],
+            recv_sem=recv_sem.at[step],
+            device_id=peer,
+            device_id_type=MESH,
+        )
+        copy.start()
+        copy.wait()
+        totals[step + 1] = totals[step] + heard[step]
+
+
+def gather_kernel(
+    n_rep,
+    count_ref,
+    in_q,
+    in_o,
+    in_k,
+    in_v,
+    count_out,
+    out_q,
+    out_o,
+    out_k,
+    out_v,
+    own_q,
+    own_o,
+    own_k,
+    own_v,
+    totals,
+    heard,
+    bf_send,
+    bf_recv,
+    load_sem,
+    send_z,
+    recv_z,
+    send_y,
+    recv_y,
+    send_c,
+    recv_c,
+):
+    section, shard, replica = place()
+    ins = (in_q, in_o, in_k, in_v)
+    outs = (out_q, out_o, out_k, out_v)
+    owns = (own_q, own_o, own_k, own_v)
+    quarter_rows = in_q.shape[0] // 4
+    mine = lax.rem(replica, 4)
+    peers = reduce_peers(n_rep)
+    sibling = (section, shard, replica ^ 1)
+    across_y = (section, shard, replica ^ 2)
+    greet(peers)
+
+    def rows(quarter):
+        return pl.ds(pl.multiple_of(quarter * quarter_rows, 128), quarter_rows)
+
+    def piece(index, source, quarter):
+        width = ins[index].shape[1]
+        return outs[index].at[rows(quarter), pl.ds(pl.multiple_of(source * width, 128), width)]
+
+    def along_z(index, source, step):
+        side = (step + 1) // 2
+        from_ref = piece(index, source, mine)
+        return pltpu.make_async_remote_copy(
+            src_ref=from_ref,
+            dst_ref=from_ref,
+            send_sem=send_z.at[side, index, source],
+            recv_sem=recv_z.at[index, source],
+            device_id=(section, shard + step, replica),
+            device_id_type=MESH,
+        )
+
+    def first_z(index, step):
+        side = (step + 1) // 2
+        return pltpu.make_async_remote_copy(
+            src_ref=ins[index].at[rows(mine), :],
+            dst_ref=piece(index, shard, mine),
+            send_sem=send_z.at[side, index, shard],
+            recv_sem=recv_z.at[index, shard],
+            device_id=(section, shard + step, replica),
+            device_id_type=MESH,
+        )
+
+    def to_y(index, source, quarter):
+        ref = piece(index, source, quarter)
+        return pltpu.make_async_remote_copy(
+            src_ref=ref,
+            dst_ref=ref,
+            send_sem=send_y.at[index, source],
+            recv_sem=recv_y.at[index, source],
+            device_id=across_y,
+            device_id_type=MESH,
+        )
+
+    def to_core(index, source, quarter, which):
+        ref = piece(index, source, quarter)
+        return pltpu.make_async_remote_copy(
+            src_ref=ref,
+            dst_ref=ref,
+            send_sem=send_c.at[which, index, source],
+            recv_sem=recv_c.at[which, index, source],
+            device_id=sibling,
+            device_id_type=MESH,
+        )
+
+    for index in range(4):
+        for step in (-1, 1):
+
+            @pl.when((shard + step >= 0) & (shard + step < 4))
+            def _():
+                first_z(index, step).start()
+
+    loads = [
+        pltpu.make_async_copy(ins[index], owns[index], load_sem.at[index]) for index in range(4)
+    ]
+    for load in loads:
+        load.start()
+    totals[0] = count_ref[...]
+    butterfly(peers, totals, heard, bf_send, bf_recv)
+    count_out[...] = totals[len(peers)]
+    stores = []
+    for index in range(4):
+        loads[index].wait()
+        width = ins[index].shape[1]
+        store = pltpu.make_async_copy(
+            owns[index],
+            outs[index].at[:, pl.ds(pl.multiple_of(shard * width, 128), width)],
+            load_sem.at[index],
+        )
+        store.start()
+        stores.append(store)
+
+    items = [(d, index, side) for d in (1, 2, 3) for index in range(4) for side in (-1, 1)]
+    for place_in_line in range(len(items) + 1):
+        if place_in_line < len(items):
+            d, index, side = items[place_in_line]
+            source = shard + side * d
+
+            @pl.when((source >= 0) & (source < 4))
+            def _():
+                along_z(index, source, -side).wait_recv()
+
+                @pl.when((shard - side >= 0) & (shard - side < 4))
+                def _():
+                    along_z(index, source, -side).start()
+
+                to_y(index, source, mine).start()
+                to_core(index, source, mine, 0).start()
+
+        if place_in_line > 0:
+            d, index, side = items[place_in_line - 1]
+            source = shard + side * d
+
+            @pl.when((source >= 0) & (source < 4))
+            def _():
+                to_y(index, source, mine ^ 2).wait_recv()
+                to_core(index, source, mine ^ 2, 1).start()
+
+    for d, index, side in items:
+        source = shard + side * d
+
+        @pl.when((source >= 0) & (source < 4))
+        def _():
+            to_core(index, source, mine ^ 1, 0).wait_recv()
+            to_core(index, source, mine ^ 3, 1).wait_recv()
+            to_y(index, source, mine).wait_send()
+            to_core(index, source, mine, 0).wait_send()
+            to_core(index, source, mine ^ 2, 1).wait_send()
+
+            @pl.when((shard - side >= 0) & (shard - side < 4))
+            def _():
+                along_z(index, source, -side).wait_send()
+
+    for index in range(4):
+        for step in (-1, 1):
+
+            @pl.when((shard + step >= 0) & (shard + step < 4))
+            def _():
+                first_z(index, step).wait_send()
+
+        stores[index].wait()
+
+
+def gather_weights(n_rep, count, w_q, w_o, w_k, w_v):
+    weights = (w_q, w_o, w_k, w_v)
+    steps = n_rep.bit_length() - 1 + 2
+    bf16, f32 = jnp.bfloat16, jnp.float32
+    dma = pltpu.SemaphoreType.DMA
+    return pl.pallas_call(
+        functools.partial(gather_kernel, n_rep),
+        out_shape=(jax.ShapeDtypeStruct(count.shape, f32),)
+        + tuple(jax.ShapeDtypeStruct((w.shape[0], w.shape[1] * 4), bf16) for w in weights),
+        in_specs=[VM] + [ANY] * 4,
+        out_specs=(VM,) + (ANY,) * 4,
+        scratch_shapes=[pltpu.VMEM(w.shape, bf16) for w in weights]
+        + [
+            pltpu.VMEM((steps + 1,) + count.shape, f32),
+            pltpu.VMEM((steps,) + count.shape, f32),
+            dma((steps,)),
+            dma((steps,)),
+            dma((4,)),
+            dma((2, 4, 4)),
+            dma((4, 4)),
+            dma((4, 4)),
+            dma((4, 4)),
+            dma((2, 4, 4)),
+            dma((2, 4, 4)),
+        ],
+        compiler_params=pltpu.CompilerParams(
+            collective_id=0, has_side_effects=True, vmem_limit_bytes=16 << 20
+        ),
+        name="gather_weights",
+    )(count, *weights)
+
+
+def sum_kernel(n_rep, part_ref, group_out, whole_out, totals, heard, send_sem, recv_sem):
+    section, shard, replica = place()
+    peers = reduce_peers(n_rep) + [(1 - section, shard, replica)]
+    greet(peers)
+    totals[0] = part_ref[...]
+    butterfly(peers, totals, heard, send_sem, recv_sem)
+    group_out[...] = totals[len(peers) - 1]
+    whole_out[...] = totals[len(peers)]
+
+
+def small_sums(n_rep, part):
+    steps = n_rep.bit_length() - 1 + 3
+    shape = jax.ShapeDtypeStruct(part.shape, jnp.float32)
+    return pl.pallas_call(
+        functools.partial(sum_kernel, n_rep),
+        out_shape=(shape, shape),
+        in_specs=[VM],
+        out_specs=(VM, VM),
+        scratch_shapes=[
+            pltpu.VMEM((steps + 1,) + part.shape, jnp.float32),
+            pltpu.VMEM((steps,) + part.shape, jnp.float32),
+            pltpu.SemaphoreType.DMA((steps,)),
+            pltpu.SemaphoreType.DMA((steps,)),
+        ],
+        compiler_params=pltpu.CompilerParams(
+            collective_id=1, has_side_effects=True, vmem_limit_bytes=8 << 20
+        ),
+        name="small_sums",
+    )(part)
+
+
+def flip(block, bit):
+    size = lax.axis_size("replica")
+    return lax.ppermute(block, "replica", [(i, i ^ bit) for i in range(size)])
+
+
+def owned(left, right, split):
+    size = lax.axis_size("replica")
+    me = lax.axis_index("replica")
+    divided = right if split else left
+    length = divided.shape[1] // size
+    blocks = divided.reshape(divided.shape[0], size // 2, 2, length)
+
+    def product(which):
+        chosen = lax.dynamic_index_in_dim(blocks, which, 2, keepdims=False)
+        chosen = chosen.reshape(divided.shape[0], -1)
+        if split:
+            total = down_rows(left, chosen)
+            return total
+        return down_rows(chosen, right)
+
+    sent = product(1 - (me & 1)).astype(jnp.bfloat16)
+    arrived = flip(sent, 1)
+    total = product(me & 1) + arrived.astype(jnp.float32)
+    bit = 2
+    while bit < size:
+        here = (me // bit) & 1
+        if split:
+            halves = total.reshape(total.shape[0], -1, 2, length)
+        else:
+            halves = total.reshape(-1, 2, length, total.shape[1])
+        axis = 2 if split else 1
+        away = lax.dynamic_index_in_dim(halves, 1 - here, axis, keepdims=False)
+        keep = lax.dynamic_index_in_dim(halves, here, axis, keepdims=False)
+        arrived = flip(away.astype(jnp.bfloat16), bit)
+        total = keep + arrived.astype(jnp.float32)
+        total = total.reshape((total.shape[0], -1) if split else (-1, total.shape[-1]))
+        bit *= 2
+    return total
+
+
+def over_shard(grad):
+    return lax.psum_scatter(
+        grad.astype(jnp.bfloat16), "shard", scatter_dimension=1, tiled=True
     ).astype(jnp.float32)
-    if split_more:
-        portion = lax.psum_scatter(
-            portion.astype(jnp.bfloat16), "shard", scatter_dimension=1, tiled=True
-        ).astype(jnp.float32)
-    return portion
 
 
 def per_device(
@@ -104,6 +416,7 @@
 ):
     f32 = jnp.float32
     bf16 = jnp.bfloat16
+    n_rep = lax.axis_size("replica")
     section_id = lax.axis_index("section")
     later = section_id == 1
     micro_count = lengths.shape[0]
@@ -116,16 +429,19 @@
     teacher = targets[arrival].astype(f32)
     gain_attn = attn_gain[0].astype(f32)
     gain_ffn = ffn_gain[0].astype(f32)
-    w_q, w_k, w_v, w_o = (
-        lax.all_gather(w_query[0], "shard", axis=1, tiled=True),
-        lax.all_gather(w_key[0], "shard", axis=1, tiled=True),
-        lax.all_gather(w_value[0], "shard", axis=1, tiled=True),
-        lax.all_gather(w_out[0], "shard", axis=1, tiled=True),
-    )
+    local_count = jnp.broadcast_to(jnp.sum(lengths).astype(f32), (8, 128))
+    counted, w_q, w_o, w_k, w_v = gather_weights(
+        n_rep, local_count, w_query[0], w_out[0], w_key[0], w_value[0]
+    )
+    total_count = counted[0, 0]
     w_g, w_u, w_d = (w_gate[0], w_up[0], w_down[0])
     received = jnp.zeros((row_count, model_width), bf16)
     outputs_seen = []
     kept_seen = []
+
+    def pick(one, zero):
+        return jax.tree.map(lambda a, b: jnp.where(later, a, b), one, zero)
+
     for moment in range(micro_count + 1):
         own_batch = jnp.clip(moment - section_id, 0, micro_count - 1)
         fresh = lax.dynamic_index_in_dim(slot_inputs, own_batch, 0, keepdims=False)
@@ -192,8 +508,8 @@
             forward_hidden,
             forward_inverse_two,
             ffn_spread,
-            ffn_gate_pre,
-            ffn_up_pre,
+            ffn_gate_pre.astype(bf16),
+            ffn_up_pre.astype(bf16),
             ffn_active,
         )
         result = forward_hidden + branch
@@ -202,24 +518,18 @@
             received = from_behind(result.astype(bf16), "section", 1)
         outputs_seen.append(result)
         kept_seen.append(kept)
-    mine = lax.dynamic_slice_in_dim(jnp.stack(outputs_seen), section_id, micro_count, 0).reshape(
-        -1, model_width
+    mine = jnp.concatenate(
+        [pick(outputs_seen[batch + 1], outputs_seen[batch]) for batch in range(micro_count)]
     )
     segments_all = jax.vmap(lambda seq_lengths: layout(seq_lengths, row_count)[0])(lengths)
     valid_rows = (segments_all < lengths.shape[1]).reshape(-1).astype(f32)[:, None]
     errors = mine - teacher
     switch = later.astype(f32)
     local_square = jnp.sum(valid_rows * errors * errors) * switch
-    local_count = jnp.sum(lengths).astype(f32) * switch
-    total_square, total_count = lax.psum(
-        (local_square, local_count), ("section", "shard", "replica")
-    )
-    loss_value = total_square / (total_count * model_width)
     all_tokens = tokens.shape[0] * lax.axis_size("shard") * lax.axis_size("replica")
     grad_final = (all_tokens / total_count * errors * valid_rows).reshape(
         micro_count, row_count, model_width
     )
-    stacked_kept = jax.tree.map(lambda *pieces: jnp.stack(pieces), *kept_seen)
     coming = jnp.zeros((row_count, model_width), bf16)
     sent_seen = []
     stored_seen = []
@@ -228,12 +538,10 @@
     for moment in range(micro_count + 1):
         raw_batch = moment - 1 + section_id
         own_batch = jnp.clip(raw_batch, 0, micro_count - 1)
-        kept = jax.tree.map(
-            lambda arrays: lax.dynamic_index_in_dim(
-                arrays, own_batch + section_id, 0, keepdims=False
-            ),
-            stacked_kept,
-        )
+        if moment == 1:
+            kept = pick(kept_seen[2], kept_seen[0])
+        else:
+            kept = kept_seen[1]
         seq_lengths = lax.dynamic_index_in_dim(lengths, own_batch, 0, keepdims=False)
         final_rows = lax.dynamic_index_in_dim(grad_final, own_batch, 0, keepdims=False)
         incoming = jnp.where(later, final_rows, coming.astype(f32))
@@ -253,6 +561,7 @@
             up_pre,
             active,
         ) = kept
+        gate_pre, up_pre = gate_pre.astype(f32), up_pre.astype(f32)
         allowed, cosine, sine = attend_mask(seq_lengths, row_count)
         grad_branch = incoming.astype(bf16)
         backward_grad_rows = lax.all_gather(grad_branch, "shard", axis=0, tiled=True)
@@ -330,30 +639,21 @@
             backward_grad_rows,
             active,
         )
-        grad_input, stored, gain_attn_part, gain_ffn_part = (
-            grad_input,
-            stored,
-            gain_attn_part,
-            gain_ffn_part,
-        )
-        active_moment = ((raw_batch >= 0) & (raw_batch < micro_count)).astype(f32)
-        gain_attn_total = gain_attn_total + active_moment * gain_attn_part
-        gain_ffn_total = gain_ffn_total + active_moment * gain_ffn_part
+        active_moment = (raw_batch >= 0) & (raw_batch < micro_count)
+        gain_attn_total = gain_attn_total + jnp.where(active_moment, gain_attn_part, 0.0)
+        gain_ffn_total = gain_ffn_total + jnp.where(active_moment, gain_ffn_part, 0.0)
         sent = grad_input.astype(bf16)
         if moment < micro_count:
             coming = from_behind(sent, "section", -1)
         sent_seen.append(sent)
         stored_seen.append(stored)
-    first_moment = 1 - section_id
-    grads_in = lax.dynamic_slice_in_dim(jnp.stack(sent_seen), first_moment, micro_count, 0).reshape(
-        -1, model_width
-    )
-    stacked_stored = jax.tree.map(lambda *pieces: jnp.stack(pieces), *stored_seen)
+    grads_in = jnp.concatenate(
+        [pick(sent_seen[batch], sent_seen[batch + 1]) for batch in range(micro_count)]
+    )
     stored_valid = jax.tree.map(
-        lambda arrays: lax.dynamic_slice_in_dim(arrays, first_moment, micro_count, 0).reshape(
-            (-1,) + arrays.shape[2:]
-        ),
-        stacked_stored,
+        lambda both, other: jnp.concatenate([both, other]),
+        stored_seen[1],
+        pick(stored_seen[0], stored_seen[2]),
     )
     (
         normed_rows,
@@ -368,17 +668,21 @@
         grad_rows,
         active_rows,
     ) = stored_valid
-    query_grad = owned(down_rows(normed_rows, grad_query), True)
-    key_grad = owned(down_rows(normed_rows, grad_keys), True)
-    value_grad = owned(down_rows(normed_rows, grad_values), True)
-    out_grad = owned(down_rows(mixed_rows, grad_attn), True)
-    gate_grad = owned(down_rows(spread_rows, grad_gate), False)
-    up_grad = owned(down_rows(spread_rows, grad_up), False)
-    down_grad = owned(down_rows(grad_rows, active_rows), False).T
-    attn_gain_part, ffn_gain_part = (
-        lax.psum_scatter(gain_attn_total, ("shard", "replica"), scatter_dimension=0, tiled=True),
-        lax.psum_scatter(gain_ffn_total, ("shard", "replica"), scatter_dimension=0, tiled=True),
-    )
+    down_grad = owned(active_rows, grad_rows, 1)
+    gate_grad = owned(spread_rows, grad_gate, 0)
+    up_grad = owned(spread_rows, grad_up, 0)
+    out_grad = over_shard(owned(mixed_rows, grad_attn, 0))
+    query_grad = over_shard(owned(normed_rows, grad_query, 0))
+    key_grad = over_shard(owned(normed_rows, grad_keys, 0))
+    value_grad = over_shard(owned(normed_rows, grad_values, 0))
+    small = jnp.stack([gain_attn_total, gain_ffn_total])
+    small = jnp.concatenate([small, jnp.broadcast_to(local_square, (6, model_width))])
+    group_sums, whole_sums = small_sums(n_rep, small)
+    loss_value = whole_sums[2, 0] / (total_count * model_width)
+    share = model_width // (lax.axis_size("shard") * n_rep)
+    start = (lax.axis_index("shard") * n_rep + lax.axis_index("replica")) * share
+    attn_gain_part = lax.dynamic_slice_in_dim(group_sums[0], start, share, 0)
+    ffn_gain_part = lax.dynamic_slice_in_dim(group_sums[1], start, share, 0)
     outputs_local = (
         jnp.zeros((tokens.shape[0], model_width), bf16).at[arrival].set(mine.astype(bf16))[None]
     )

time: 1790 us -> 1320 us (0.74)
  waiting for transfers between devices: 1160 us -> 502 us
  Pallas kernels: 0 us -> 204 us
  blocking collectives: 99.3 us -> 0 us
  local copies, waits for them, and re-layouts: 84.8 us -> 181 us
  matrix products: 296 us -> 276 us
    reduce_scatter x9 -> x2, waiting for transfers between devices: 372 us -> 0.01 us  [over_shard(): lax.psum_scatter(grad.astype(jnp.bfloat16), 'shard', scatter_dimension=1,...]
    all_gather x4 -> x0, waiting for transfers between devices: 361 us -> none  [the longest x1 146 us: per_device(): lax.all_gather(w_query[0], 'shard', axis=1, tiled=True)]
    pallas_call x0 -> x2, Pallas kernels: none -> 204 us  [the longest x1 139 us: gather_weights(): pl.pallas_call(functools.partial(gather_kernel, n_rep), out_shape=(jax.Sh...]
    ppermute x0 -> x14, waiting for transfers between devices: none -> 122 us  [flip(): return lax.ppermute(block, 'replica', [(i, i ^ bit) for i in range(size)])]
    unnamed x1 -> x0, blocking collectives: 60.3 us -> none
    unnamed x416 -> x465, local copies, waits for them, and re-layouts: 33 us -> 81.6 us
    another operation x36 -> x19, other arithmetic: 50.1 us -> 8.44 us  [the longest x15 33.2 us: per_device(): stacked_kept = jax.tree.map(lambda *pieces: jnp.stack(pieces), *kept_seen)]
    psum x1 -> x0, blocking collectives: 39 us -> none  [per_device(): lax.psum((local_square, local_count), ('section', 'shard', 'replica'))]
  transfers between devices with their start and end apart: 31 -> 34, of which waited for: 28 -> 19; matrix products, arithmetic and copies ran while one was open for 11% -> 18% of each run, Pallas kernels for 0% -> 5%
where the time goes in v1:
time: 1320 us; the launch traced here: 1310 us
  waiting for transfers between devices  502 us (38%)
  matrix products  276 us (21%)
  Pallas kernels  204 us (15%)
  local copies, waits for them, and re-layouts  181 us (14%)
  other arithmetic  102 us (8%)
  starting transfers between devices  23.9 us (2%)
  between operations  21.9 us (2%)
    pallas_call x1, Pallas kernels, gather_weights(): pl.pallas_call(functools.partial(gather_kernel, n_rep), out_shape=(jax.Sh...  139 us
    ppermute x14, waiting for transfers between devices, flip(): return lax.ppermute(block, 'replica', [(i, i ^ bit) for i in range(size)])  122 us
    all_gather x3, waiting for transfers between devices, per_device(): ffn_spread = lax.all_gather(forward_normed_two, 'shard', axis=0, tiled=True)  109 us
    dot_general x21, matrix products, across(): lax.dot_general(left, right, (((1,), (1,)), ((), ())), preferred_element_...  108 us
    reduce_scatter x3, waiting for transfers between devices, per_device(): lax.psum_scatter(jnp.dot(ffn_active, w_d, preferred_element_type=f32).ast...  97.5 us
    unnamed x465, local copies, waits for them, and re-layouts  81.6 us
    all_gather x3, waiting for transfers between devices, per_device(): lax.all_gather(grad_branch, 'shard', axis=0, tiled=True)  71 us
    reduce_scatter x3, waiting for transfers between devices, per_device(): lax.psum_scatter((across(backward_grad_gate, w_g) + across(backward_grad_...  66.7 us
  transfers between devices with their start and end apart: 34, of which 19 were waited for; matrix products, arithmetic and copies ran while one was open for 18% of the time, Pallas kernels for 5%

profile of v1, /device:TPU:0, one launch (start us, length us, event | category | flops | bytes accessed | tf_op | source)
XLA Modules:
  0.0 1310.9 jit_solution(6707003247262768527)
XLA Ops:
  21.1 139.0 %gather_weights.1 = (f32[8,128]{1,0:T(8,128)S(1)}, bf16[2048,2048]{1,0:T(8,128)(2,1)S(1)}, bf16[2048,2048]{1,0:T(8,128)(2,1)S(1)}, bf16[2048,512]{1,0:T(8,128)(2,1)S(1)}, bf16[2048,512]{1,0:T(8,128)(2,1)S(1)}) custom-call(f32[8,128]{1,0:T(8,128)S(1)} %broadcast_in_dim.66.count_ref, bf16[2048,512]{1,0:T(8,128)(2,1)S(1)} %bitcast.556, ...), custom_call_target="tpu_custom_call" | custom-call | tf_op jit(solution)/shard_map/gather_weights/pallas_call | solution.py:298
  174.2 12.3 copy.149
  199.0 34.8 %all-gather.7.cloned.1.call-done = bf16[384,2048]{1,0:T(8,128)(2,1)} async-done(((bf16[96,2048]{1,0:T(8,128)(2,1)}), bf16[384,2048]{1,0:T(8,128)(2,1)}) %all-gather.7.cloned.1.call-update) | async-done | bytes 1572880 | tf_op jit(solution)/shard_map/all_gather | solution.py:489
  241.0 9.7 multiply_convert_fusion.2
  256.5 34.4 %reduce-scatter.15.cloned.1.call-done = bf16[96,2048]{1,0:T(8,128)(2,1)} async-done(((bf16[384,2048]{1,0:T(8,128)(2,1)}), bf16[96,2048]{1,0:T(8,128)(2,1)}) %reduce-scatter.15.cloned.1.call-update) | async-done | bytes 393232 | tf_op jit(solution)/shard_map/reduce_scatter | solution.py:493
  324.9 36.9 %all-gather.9.cloned.1.call-done = bf16[384,2048]{1,0:T(8,128)(2,1)} async-done(((bf16[96,2048]{1,0:T(8,128)(2,1)}), bf16[384,2048]{1,0:T(8,128)(2,1)}) %all-gather.9.cloned.1.call-update) | async-done | bytes 1572880 | tf_op jit(solution)/shard_map/all_gather | solution.py:489
  369.1 9.7 multiply_convert_fusion.1
  384.6 34.4 %reduce-scatter.17.cloned.1.call-done = bf16[96,2048]{1,0:T(8,128)(2,1)} async-done(((bf16[384,2048]{1,0:T(8,128)(2,1)}), bf16[96,2048]{1,0:T(8,128)(2,1)}) %reduce-scatter.17.cloned.1.call-update) | async-done | bytes 393232 | tf_op jit(solution)/shard_map/reduce_scatter | solution.py:493
  457.4 37.1 %all-gather.11.cloned.1.call-done = bf16[384,2048]{1,0:T(8,128)(2,1)} async-done(((bf16[96,2048]{1,0:T(8,128)(2,1)}), bf16[384,2048]{1,0:T(8,128)(2,1)}) %all-gather.11.cloned.1.call-update) | async-done | bytes 1572880 | tf_op jit(solution)/shard_map/all_gather | solution.py:489
  501.0 10.1 broadcast_select_fusion.1
  521.5 28.7 %reduce-scatter.19.cloned.1.call-done = bf16[96,2048]{1,0:T(8,128)(2,1)} async-done(((bf16[384,2048]{1,0:T(8,128)(2,1)}), bf16[96,2048]{1,0:T(8,128)(2,1)}) %reduce-scatter.19.cloned.1.call-update) | async-done | bytes 393232 | tf_op jit(solution)/shard_map/reduce_scatter | solution.py:493
  555.7 35.7 %all-gather.13.cloned.1.call-done = bf16[384,2048]{1,0:T(8,128)(2,1)} async-done(((bf16[96,2048]{1,0:T(8,128)(2,1)}), bf16[384,2048]{1,0:T(8,128)(2,1)}) %all-gather.13.cloned.1.call-update) | async-done | bytes 1572880 | tf_op jit(solution)/shard_map/all_gather | solution.py:567
  591.4 10.5 fusion.41
  615.8 33.8 %reduce-scatter.21.cloned.1.call-done = bf16[96,2048]{1,0:T(8,128)(2,1)} async-done(((bf16[384,2048]{1,0:T(8,128)(2,1)}), bf16[96,2048]{1,0:T(8,128)(2,1)}) %reduce-scatter.21.cloned.1.call-update) | async-done | bytes 393232 | tf_op jit(solution)/shard_map/reduce_scatter | solution.py:574
  675.5 11.1 collective-permute-done.2
  689.6 35.2 %all-gather.15.cloned.1.call-done = bf16[384,2048]{1,0:T(8,128)(2,1)} async-done(((bf16[96,2048]{1,0:T(8,128)(2,1)}), bf16[384,2048]{1,0:T(8,128)(2,1)}) %all-gather.15.cloned.1.call-update) | async-done | bytes 1572880 | tf_op jit(solution)/shard_map/all_gather | solution.py:567
  724.8 10.5 fusion.50
  750.0 32.9 %reduce-scatter.23.cloned.1.call-done = bf16[96,2048]{1,0:T(8,128)(2,1)} async-done(((bf16[384,2048]{1,0:T(8,128)(2,1)}), bf16[96,2048]{1,0:T(8,128)(2,1)}) %reduce-scatter.23.cloned.1.call-update) | async-done | bytes 393232 | tf_op jit(solution)/shard_map/reduce_scatter | solution.py:574
  811.1 11.0 collective-permute-done.3
  839.1 12.0 constant_dynamic-slice_fusion.5
  851.1 8.2 copy.220
  859.4 8.2 copy.221
  889.3 11.4 broadcast_select_fusion.3
  906.6 10.2 add_convert_fusion
  927.3 12.0 constant_dynamic-slice_fusion.3
  939.4 8.2 copy.222
  947.5 8.1 copy.223
  1030.0 64.7 %small_sums.1 = (f32[8,2048]{1,0:T(8,128)S(1)}, f32[8,2048]{1,0:T(8,128)S(1)}) custom-call(f32[8,2048]{1,0:T(8,128)S(1)} %maximum_maximum_fusion.part_ref), custom_call_target="tpu_custom_call" | custom-call | tf_op jit(solution)/shard_map/small_sums/pallas_call | solution.py:338
  1136.5 24.8 %collective-permute-done.11 = bf16[1,512,2048]{2,1,0:T(8,128)(2,1)S(1)} collective-permute-done((bf16[1,512,2048]{2,1,0:T(8,128)(2,1)S(1)}, bf16[1,512,2048]{2,1,0:T(8,128)(2,1)S(1)}, u32[]{:S(2)}, u32[]{:S(2)}) %collective-permute-start.11) | collective-permute-done | bytes 2097184 | tf_op jit(solution)/shard_map/ppermute | solution.py:358
  1192.9 13.5 %collective-permute-done.13 = bf16[1,512,2048]{2,1,0:T(8,128)(2,1)} collective-permute-done((bf16[1,512,2048]{2,1,0:T(8,128)(2,1)}, bf16[1,512,2048]{2,1,0:T(8,128)(2,1)}, u32[]{:S(2)}, u32[]{:S(2)}) %collective-permute-start.13) | collective-permute-done | bytes 2097184 | tf_op jit(solution)/shard_map/ppermute | solution.py:358
  1212.1 39.2 %collective-permute-done.15 = bf16[1,512,2048]{2,1,0:T(8,128)(2,1)} collective-permute-done((bf16[1,512,2048]{2,1,0:T(8,128)(2,1)}, bf16[1,512,2048]{2,1,0:T(8,128)(2,1)}, u32[]{:S(2)}, u32[]{:S(2)}) %collective-permute-start.15) | collective-permute-done | bytes 2097184 | tf_op jit(solution)/shard_map/ppermute | solution.py:358
  1257.2 38.5 %collective-permute-done.17 = bf16[2048,1,512]{2,0,1:T(8,128)(2,1)S(1)} collective-permute-done((bf16[2048,1,512]{2,0,1:T(8,128)(2,1)}, bf16[2048,1,512]{2,0,1:T(8,128)(2,1)S(1)}, u32[]{:S(2)}, u32[]{:S(2)}) %collective-permute-start.17) | collective-permute-done | bytes 2097184 | tf_op jit(solution)/shard_map/ppermute | solution.py:358
  (773 shorter events, 462.2 us)
Async XLA Ops:
  7.2 226.6 %all-gather.7.cloned.1.call-start = ((), (), s32[]{:S(2)}) async-start(), calls=%async_computation.10 | async-start | bytes 1966080 | tf_op jit(solution)/shard_map/all_gather | solution.py:489
  198.8 92.2 %reduce-scatter.15.cloned.1.call-start = ((), (), s32[]{:S(2)}) async-start(), calls=%async_computation.11 | async-start | bytes 1966080 | tf_op jit(solution)/shard_map/reduce_scatter | solution.py:493
  256.5 105.3 %all-gather.9.cloned.1.call-start = ((), (), s32[]{:S(2)}) async-start(), calls=%async_computation.12 | async-start | bytes 1966080 | tf_op jit(solution)/shard_map/all_gather | solution.py:489
  324.4 94.6 %reduce-scatter.17.cloned.1.call-start = ((), (), s32[]{:S(2)}) async-start(), calls=%async_computation.13 | async-start | bytes 1966080 | tf_op jit(solution)/shard_map/reduce_scatter | solution.py:493
  384.6 109.9 %all-gather.11.cloned.1.call-start = ((), (), s32[]{:S(2)}) async-start(), calls=%async_computation.14 | async-start | bytes 1966080 | tf_op jit(solution)/shard_map/all_gather | solution.py:489
  457.1 93.0 %reduce-scatter.19.cloned.1.call-start = ((), (), s32[]{:S(2)}) async-start(), calls=%async_computation.15 | async-start | bytes 1966080 | tf_op jit(solution)/shard_map/reduce_scatter | solution.py:493
  515.7 75.7 %all-gather.13.cloned.1.call-start = ((), (), s32[]{:S(2)}) async-start(), calls=%async_computation.16 | async-start | bytes 1966080 | tf_op jit(solution)/shard_map/all_gather | solution.py:567
  555.4 94.2 %reduce-scatter.21.cloned.1.call-start = ((), (), s32[]{:S(2)}) async-start(), calls=%async_computation.17 | async-start | bytes 1966080 | tf_op jit(solution)/shard_map/reduce_scatter | solution.py:574
  615.1 109.7 %all-gather.15.cloned.1.call-start = ((), (), s32[]{:S(2)}) async-start(), calls=%async_computation.18 | async-start | bytes 1966080 | tf_op jit(solution)/shard_map/all_gather | solution.py:567
  674.2 12.4 collective-permute-start.2
  689.4 93.5 %reduce-scatter.23.cloned.1.call-start = ((), (), s32[]{:S(2)}) async-start(), calls=%async_computation.19 | async-start | bytes 1966080 | tf_op jit(solution)/shard_map/reduce_scatter | solution.py:574
  748.4 140.9 %all-gather.17.cloned.1.call-start = ((), (), s32[]{:S(2)}) async-start(), calls=%async_computation.20 | async-start | bytes 1966080 | tf_op jit(solution)/shard_map/all_gather | solution.py:567
  809.8 12.3 collective-permute-start.3
  824.9 149.4 %reduce-scatter.25.cloned.1.call-start = ((), (), s32[]{:S(2)}) async-start(), calls=%async_computation.21 | async-start | bytes 1966080 | tf_op jit(solution)/shard_map/reduce_scatter | solution.py:574
  916.8 272.5 %reduce-scatter.33.cloned.1.call-start = ((), (), s32[]{:S(2)}) async-start(), calls=%async_computation.25 | async-start | bytes 655360
  963.6 150.7 %collective-permute-start.12 = (bf16[1024,2048]{1,0:T(8,128)(2,1)}, bf16[1024,2048]{1,0:T(8,128)(2,1)}, u32[]{:S(2)}, u32[]{:S(2)}) collective-permute-start(bf16[1024,2048]{1,0:T(8,128)(2,1)} %convolution_convert_fusion.4), channel_id=1, source_target_pairs={{0,1},{1,0},{2,3},{3,2},{4,5},{5,4},{6,7},{7,6},{8,9},{9,8},{10,11... | collective-permute-start | bytes 12582920 | tf_op jit(solution)/shard_map/ppermute | solution.py:358
  968.6 154.4 %collective-permute-start.14 = (bf16[1024,2048]{1,0:T(8,128)(2,1)}, bf16[1024,2048]{1,0:T(8,128)(2,1)}, u32[]{:S(2)}, u32[]{:S(2)}) collective-permute-start(bf16[1024,2048]{1,0:T(8,128)(2,1)} %convolution_convert_fusion.3), channel_id=1, source_target_pairs={{0,1},{1,0},{2,3},{3,2},{4,5},{5,4},{6,7},{7,6},{8,9},{9,8},{10,11... | collective-permute-start | bytes 12582920 | tf_op jit(solution)/shard_map/ppermute | solution.py:358
  996.9 15.1 %collective-permute-start.4 = (bf16[1024,2048]{1,0:T(8,128)(2,1)S(1)}, bf16[1024,2048]{1,0:T(8,128)(2,1)S(1)}, u32[]{:S(2)}, u32[]{:S(2)}) collective-permute-start(bf16[1024,2048]{1,0:T(8,128)(2,1)S(1)} %convolution_convert_fusion.1), channel_id=1, source_target_pairs={{0,1},{1,0},{2,3},{3,2},{4,5},{5,4},{6,7},{7,6},{8,9},{9,8},{10,11... | collective-permute-start | bytes 12582920 | tf_op jit(solution)/shard_map/ppermute | solution.py:358
  998.2 13.1 collective-permute-start.8
  999.9 20.1 %collective-permute-start.6 = (bf16[1024,512]{1,0:T(8,128)(2,1)S(1)}, bf16[1024,512]{1,0:T(8,128)(2,1)S(1)}, u32[]{:S(2)}, u32[]{:S(2)}) collective-permute-start(bf16[1024,512]{1,0:T(8,128)(2,1)S(1)} %convolution_convert_fusion.9), channel_id=1, source_target_pairs={{0,1},{1,0},{2,3},{3,2},{4,5},{5,4},{6,7},{7,6},{8,9},{9,8},{10,11... | collective-permute-start | bytes 3145736 | tf_op jit(solution)/shard_map/ppermute | solution.py:358
  1011.3 96.9 %collective-permute-start.10 = (bf16[1024,2048]{1,0:T(8,128)(2,1)}, bf16[1024,2048]{1,0:T(8,128)(2,1)}, u32[]{:S(2)}, u32[]{:S(2)}) collective-permute-start(bf16[1024,2048]{1,0:T(8,128)(2,1)} %convolution_convert_fusion), channel_id=1, source_target_pairs={{0,1},{1,0},{2,3},{3,2},{4,5},{5,4},{6,7},{7,6},{8,9},{9,8},{10,11... | collective-permute-start | bytes 12582920 | tf_op jit(solution)/shard_map/ppermute | solution.py:358
  1012.1 14.9 %collective-permute-start.9 = (bf16[1,512,512]{2,1,0:T(8,128)(2,1)S(1)}, bf16[1,512,512]{2,1,0:T(8,128)(2,1)S(1)}, u32[]{:S(2)}, u32[]{:S(2)}) collective-permute-start(bf16[1,512,512]{2,1,0:T(8,128)(2,1)S(1)} %fusion.183), channel_id=1, source_target_pairs={{0,2},{1,3},{2,0},{3,1},{4,6},{5,7},{6,4},{7,5},{8,10},{9,11},{10,... | collective-permute-start | bytes 1572872 | tf_op jit(solution)/shard_map/ppermute | solution.py:358
  1020.0 82.7 %collective-permute-start.5 = (bf16[1,512,2048]{2,1,0:T(8,128)(2,1)}, bf16[1,512,2048]{2,1,0:T(8,128)(2,1)}, u32[]{:S(2)}, u32[]{:S(2)}) collective-permute-start(bf16[1,512,2048]{2,1,0:T(8,128)(2,1)} %fusion.76), channel_id=1, source_target_pairs={{0,2},{1,3},{2,0},{3,1},{4,6},{5,7},{6,4},{7,5},{8,10},{9,11},{10,... | collective-permute-start | bytes 6291464 | tf_op jit(solution)/shard_map/ppermute | solution.py:358
  1028.2 162.2 %reduce-scatter.31.cloned.1.call-start = ((), (), s32[]{:S(2)}) async-start(), calls=%async_computation.24 | async-start | bytes 655360
  1028.3 67.6 %collective-permute-start.7 = (bf16[1,512,512]{2,1,0:T(8,128)(2,1)S(1)}, bf16[1,512,512]{2,1,0:T(8,128)(2,1)S(1)}, u32[]{:S(2)}, u32[]{:S(2)}) collective-permute-start(bf16[1,512,512]{2,1,0:T(8,128)(2,1)S(1)} %fusion.182), channel_id=1, source_target_pairs={{0,2},{1,3},{2,0},{3,1},{4,6},{5,7},{6,4},{7,5},{8,10},{9,11},{10,... | collective-permute-start | bytes 1572872 | tf_op jit(solution)/shard_map/ppermute | solution.py:358
  1095.9 67.5 %collective-permute-start.16 = (bf16[2048,1024]{0,1:T(8,128)(2,1)}, bf16[2048,1024]{0,1:T(8,128)(2,1)}, u32[]{:S(2)}, u32[]{:S(2)}) collective-permute-start(bf16[2048,1024]{0,1:T(8,128)(2,1)} %convolution_convert_fusion.2), channel_id=1, source_target_pairs={{0,1},{1,0},{2,3},{3,2},{4,5},{5,4},{6,7},{7,6},{8,9},{9,8},{10,11... | collective-permute-start | bytes 12582920 | tf_op jit(solution)/shard_map/ppermute | solution.py:358
  1098.5 200.0 %reduce-scatter.27.cloned.1.call-start = ((), (), s32[]{:S(2)}) async-start(), calls=%async_computation.22 | async-start | bytes 2621440 | tf_op jit(solution)/shard_map/reduce_scatter | solution.py:397
  1107.7 193.0 %reduce-scatter.29.cloned.1.call-start = ((), (), s32[]{:S(2)}) async-start(), calls=%async_computation.23 | async-start | bytes 2621440 | tf_op jit(solution)/shard_map/reduce_scatter | solution.py:397
  1112.7 48.6 %collective-permute-start.11 = (bf16[1,512,2048]{2,1,0:T(8,128)(2,1)S(1)}, bf16[1,512,2048]{2,1,0:T(8,128)(2,1)S(1)}, u32[]{:S(2)}, u32[]{:S(2)}) collective-permute-start(bf16[1,512,2048]{2,1,0:T(8,128)(2,1)S(1)} %fusion.77), channel_id=1, source_target_pairs={{0,2},{1,3},{2,0},{3,1},{4,6},{5,7},{6,4},{7,5},{8,10},{9,11},{10,... | collective-permute-start | bytes 6291464 | tf_op jit(solution)/shard_map/ppermute | solution.py:358
  1121.5 84.8 %collective-permute-start.13 = (bf16[1,512,2048]{2,1,0:T(8,128)(2,1)}, bf16[1,512,2048]{2,1,0:T(8,128)(2,1)}, u32[]{:S(2)}, u32[]{:S(2)}) collective-permute-start(bf16[1,512,2048]{2,1,0:T(8,128)(2,1)} %fusion.78), channel_id=1, source_target_pairs={{0,2},{1,3},{2,0},{3,1},{4,6},{5,7},{6,4},{7,5},{8,10},{9,11},{10,... | collective-permute-start | bytes 6291464 | tf_op jit(solution)/shard_map/ppermute | solution.py:358
  1135.0 116.2 %collective-permute-start.15 = (bf16[1,512,2048]{2,1,0:T(8,128)(2,1)}, bf16[1,512,2048]{2,1,0:T(8,128)(2,1)}, u32[]{:S(2)}, u32[]{:S(2)}) collective-permute-start(bf16[1,512,2048]{2,1,0:T(8,128)(2,1)} %fusion.79), channel_id=1, source_target_pairs={{0,2},{1,3},{2,0},{3,1},{4,6},{5,7},{6,4},{7,5},{8,10},{9,11},{10,... | collective-permute-start | bytes 6291464 | tf_op jit(solution)/shard_map/ppermute | solution.py:358
  1177.2 118.4 %collective-permute-start.17 = (bf16[2048,1,512]{2,0,1:T(8,128)(2,1)}, bf16[2048,1,512]{2,0,1:T(8,128)(2,1)S(1)}, u32[]{:S(2)}, u32[]{:S(2)}) collective-permute-start(bf16[2048,1,512]{2,0,1:T(8,128)(2,1)} %bitcast.612), channel_id=1, source_target_pairs={{0,2},{1,3},{2,0},{3,1},{4,6},{5,7},{6,4},{7,5},{8,10},{9,11},{10,... | collective-permute-start | bytes 6291464 | tf_op jit(solution)/shard_map/ppermute | solution.py:358
  (229 other events, 2828.1 us)
Sparse Core Ops, SparseCore 0:
  198.9 34.8 all-gather.6
  256.6 34.2 reduce-scatter.14
  324.5 37.2 all-gather.8
  384.7 34.2 reduce-scatter.16
  457.2 37.2 all-gather.10
  515.8 34.3 reduce-scatter.18
  555.5 35.8 all-gather.12
  615.2 34.2 reduce-scatter.20
  689.5 35.2 all-gather.14
  748.5 34.3 reduce-scatter.22
  825.0 35.3 all-gather.16
  916.9 34.0 reduce-scatter.24
  1028.3 20.4 reduce-scatter.32
  1098.6 20.2 reduce-scatter.30
  1121.0 41.8 reduce-scatter.26
  1165.0 42.8 reduce-scatter.28
